TPU v7x, 32 devices: a whole 2x2x4 slice. The times are simulated.
32 devices in a mesh: blk: 16 (over z, y, x), grp: 2 (over core).
Axes of the slice: x: 2, y: 2, z: 4, core: 2. Of those that a mesh axis runs over, the one named last changes fastest.
Arguments:
- text: bfloat16 [16, 384, 1024], P('blk', 'grp'), may hold values from -64 to 64
- image: bfloat16 [16, 384, 1024], P('blk', 'grp'), may hold values from -64 to 64
- pair_index: int32 [16, 384], P('blk', 'grp'), may hold values from 0 to 383, each once within a row
Outputs:
- grad_text: float32 [16, 384, 1024], P('blk', 'grp')
- grad_image: float32 [16, 384, 1024], P('blk', 'grp')
- loss: float32 [], replicated
Inputs may be any that keep to these rules, and one draw needn't show every extreme that they name: Every sub-batch's row of pair_index names each of 0 to 383 once.
All inputs are finite; a program needn't handle non-finite values.
Results may differ from a plain program's by a relative error of at most 0.0024.
Values may be sent and summed in bfloat16 or wider, within the bound.
A program may use at most 64 MiB of HBM per device.

v0:
```python
import jax
import jax.numpy as jnp
from jax import lax
from jax.sharding import PartitionSpec as P

score_scale = 0.125


def merged(value, axis, join):
    pieces = jax.tree.map(lambda part: lax.all_gather(part, axis), value)
    head = jax.tree.map(lambda part: part[0], pieces)
    tail = jax.tree.map(lambda part: part[1:], pieces)
    so_far, _ = lax.scan(lambda so_far, piece: (join(so_far, piece), None), head, tail)
    return so_far


def join_stats(left, right):
    top = jnp.maximum(left[0], right[0])
    return (top, left[1] * jnp.exp(left[0] - top) + right[1] * jnp.exp(right[0] - top))


def local(text, image, pair_index):
    local_text = text[0]
    own_image = image[0]
    pairs = pair_index[0]
    rows = local_text.shape[0]
    total = rows * lax.axis_size("grp")
    offset = lax.axis_index("grp") * rows

    def scores_of(block):
        return (
            jnp.einsum("rd,nd->rn", local_text, block, preferred_element_type=jnp.float32)
            * score_scale
        )

    def hits_of(count):
        ids = jnp.arange(count, dtype=jnp.int32)
        return pairs[:, None] == ids[None, :]

    start_carry = (
        jnp.full((rows,), -1e30, jnp.float32),
        jnp.zeros((rows,), jnp.float32),
        jnp.zeros((total,), jnp.float32),
        jnp.zeros((total,), jnp.float32),
        jnp.zeros((rows,), jnp.float32),
    )
    block = lax.all_gather(image, "grp", axis=1, tiled=True)[0]
    count = block.shape[0]
    scores = scores_of(block)
    row_top = jnp.maximum(start_carry[0], jnp.max(scores, axis=1))
    row_total = jnp.sum(jnp.exp(scores - row_top[:, None]), axis=1)
    col_top = jnp.max(scores, axis=0)
    col_total = jnp.sum(jnp.exp(scores - col_top[None, :]), axis=0)
    col_tops = col_top
    col_totals = col_total
    positive = jnp.sum(jnp.where(hits_of(count), scores, 0.0), axis=1)
    result = (row_top, row_total, col_tops, col_totals, positive)
    carried = result
    row_lse = carried[0] + jnp.log(carried[1])
    positive = carried[4]
    col_top, col_total = merged((carried[2], carried[3]), "grp", join_stats)
    col_lse = col_top + jnp.log(col_total)
    block = lax.all_gather(image, "grp", axis=1, tiled=True)[0]
    count = block.shape[0]
    scores = scores_of(block)
    weight = (
        jnp.exp(scores - row_lse[:, None])
        + jnp.exp(scores - col_lse[None, :])
        - 2.0 * hits_of(count).astype(jnp.float32)
    ).astype(jnp.bfloat16)
    result = (jnp.dot(weight, block, preferred_element_type=jnp.float32),)
    grad_text = result[0] * (score_scale * 0.5)
    all_lse, pair_values = (
        lax.all_gather(row_lse, "grp", axis=0, tiled=True),
        lax.all_gather(pairs.astype(jnp.float32), "grp", axis=0, tiled=True),
    )
    all_pairs = pair_values.astype(jnp.int32)
    own_ids = offset + jnp.arange(rows, dtype=jnp.int32)
    own_col = lax.dynamic_slice_in_dim(col_lse, offset, rows, 0)
    piece = lax.all_gather(local_text, "grp", axis=0, tiled=True)
    count = piece.shape[0]
    flipped = (
        jnp.einsum("nd,kd->nk", own_image, piece, preferred_element_type=jnp.float32) * score_scale
    )
    hit_back = (all_pairs[None, :] == own_ids[:, None]).astype(jnp.float32)
    weight_back = (
        jnp.exp(flipped - all_lse[None, :]) + jnp.exp(flipped - own_col[:, None]) - 2.0 * hit_back
    ).astype(jnp.bfloat16)
    summed = jnp.dot(weight_back, piece, preferred_element_type=jnp.float32)
    grad_image = summed * (score_scale * 0.5)
    own_lse = lax.dynamic_slice_in_dim(col_lse, offset, rows, 0)
    partial_sum = jnp.sum(row_lse - 2.0 * positive) + jnp.sum(own_lse)
    loss = lax.psum(partial_sum, ("blk", "grp")) / (2.0 * total * lax.axis_size("blk"))
    return (grad_text[None], grad_image[None], loss)


def solution(mesh):
    placed = (P("blk", "grp", None), P("blk", "grp", None), P("blk", "grp"))
    return jax.shard_map(
        local,
        mesh=mesh,
        in_specs=placed,
        out_specs=(P("blk", "grp", None), P("blk", "grp", None), P()),
        check_vma=False,
    )
```

profile of v0, /device:TPU:0, one launch (start us, length us, event | category | flops | bytes accessed | tf_op | source)
XLA Modules:
  0.0 65.1 jit_solution(14665124273188576810)
XLA Ops:
  0.6 0.0 copy-start.3
  0.6 0.6 copy-done.3
  1.3 0.6 dynamic-slice
  2.5 0.0 copy-start.2
  2.6 0.7 %copy-done.2 = s32[1,192]{1,0:T(1,128)S(1)} copy-done((s32[1,192]{1,0:T(1,128)S(1)}, s32[1,192]{1,0:T(1,128)}, u32[]{:S(2)}) %copy-start.2) | copy-done | bytes 792
  3.2 0.1 convert_dynamic-update-slice_fusion
  3.3 0.0 copy-start
  3.3 2.8 %all_gather.25 = bf16[1,384,1024]{2,1,0:T(8,128)(2,1)S(1)} all-gather(bf16[1,192,1024]{2,1,0:T(8,128)(2,1)} %param.4), channel_id=1, replica_groups=mesh['blk'=16,'grp'=2] {'grp'}, dimensions={1}, use_global_device_ids=true | all-gather | bytes 1179648 | tf_op jit(solution)/shard_map/all_gather | solution.py:63
  6.1 0.0 copy-done
  6.1 0.5 fusion.43
  6.7 0.3 select_reduce_fusion
  7.0 0.6 subtract_reduce_fusion
  7.6 0.2 dynamic-update-slice
  7.8 2.5 %all-reduce.2 = (f32[384]{0:T(512)S(1)}, f32[384]{0:T(512)S(1)}) all-reduce(f32[384]{0:T(512)S(1)} %convert_dynamic-update-slice_fusion, f32[384]{0:T(512)S(1)} %dynamic-update-slice), channel_id=1, replica_groups=mesh['blk'=16,'grp'=2] {'grp'}, use_global_device_ids=true, to_apply=%add.1 | all-reduce | flops 768 | bytes 6144
  10.3 1.8 %all-gather.3 = f32[2,1,384]{2,1,0:T(1,128)S(1)} all-gather(f32[1,1,384]{2,1,0:T(1,128)S(1)} %reshape.41), channel_id=2, replica_groups=mesh['blk'=16,'grp'=2] {'grp'}, dimensions={0}, use_global_device_ids=true | all-gather | bytes 4608 | tf_op jit(solution)/shard_map/all_gather | solution.py:10
  12.1 1.8 %all-gather.4 = f32[2,1,384]{2,1,0:T(1,128)S(1)} all-gather(f32[1,1,384]{2,1,0:T(1,128)S(1)} %reshape.43), channel_id=3, replica_groups=mesh['blk'=16,'grp'=2] {'grp'}, dimensions={0}, use_global_device_ids=true | all-gather | bytes 4608 | tf_op jit(solution)/shard_map/all_gather | solution.py:10
  13.9 1.3 %fusion.1 = f32[1,192,1024]{2,1,0:T(8,128)} fusion(bf16[1,384,1024]{2,1,0:T(8,128)(2,1)S(1)} %all_gather.25, f32[192,384]{1,0:T(8,128)S(1)} %get-tuple-element.33, s32[192]{0:T(256)S(1)} %bitcast.73, f32[384]{0:T(512)S(1)} %fusion.37, f32[192]{0:T(256)S(1)} %get-tuple-element.32), kind=kOutput, calls=%fused_computation.3 | convolution fusion | flops 151707648 | bytes 1870848 | tf_op jit(solution)/shard_map/dot_general | solution.py:71
  15.3 0.7 %fusion.44 = (f32[]{:T(128)}, f32[192]{0:T(256)S(1)}) fusion(f32[384]{0:T(512)S(1)} %log_add_fusion, s32[]{:T(128)S(6)} %select_n.8), kind=kLoop, calls=%fused_computation.61 | loop fusion | flops 191 | bytes 1544 | tf_op jit(solution)/shard_map/reduce_sum | solution.py:92
  17.3 41.8 %psum.7 = f32[]{:T(128)} all-reduce(f32[]{:T(128)S(6)} %add.57), channel_id=1, replica_groups=mesh['blk'=16,'grp'=2] {'blk','grp'}, use_global_device_ids=true, to_apply=%region_7.8 | all-reduce | flops 1 | bytes 8 | tf_op jit(solution)/shard_map/psum | solution.py:93
  59.8 0.0 copy-start.1
  59.8 2.5 %all-gather.2 = bf16[1,384,1024]{2,1,0:T(8,128)(2,1)S(1)} all-gather(bf16[1,192,1024]{2,1,0:T(8,128)(2,1)S(1)} %copy-done), channel_id=4, replica_groups=mesh['blk'=16,'grp'=2] {'grp'}, dimensions={1}, use_global_device_ids=true | all-gather | bytes 1179648 | tf_op jit(solution)/shard_map/all_gather | solution.py:80
  62.3 0.0 copy-done.1
  62.3 1.7 %fusion = f32[1,192,1024]{2,1,0:T(8,128)} fusion(bf16[1,384,1024]{2,1,0:T(8,128)(2,1)S(1)} %all-gather.2, bf16[1,192,1024]{2,1,0:T(8,128)(2,1)S(1)} %copy-done.1, s32[384]{0:T(512)S(1)} %convert_element_type.16, f32[192]{0:T(256)S(1)} %get-tuple-element.30, f32[384]{0:T(512)S(1)} %get-tuple-element.28, s32[192]{0:T(256)S(1)} %iota_add_fusion), kind=kOutput, calls=%fused_computation.1 | convolution fusion | flops 302776320 | bytes 1970688 | tf_op jit(solution)/shard_map/dot_general | solution.py:89
  (11 shorter events, 0.1 us)
Async XLA Ops:
  0.6 0.7 %copy-start.3 = (u32[32]{0:T(128)S(1)}, u32[32]{0:T(128)}, u32[]{:S(2)}) copy-start(u32[32]{0:T(128)} %constant.40) | copy-start | bytes 388
  2.5 0.7 %copy-start.2 = (s32[1,192]{1,0:T(1,128)S(1)}, s32[1,192]{1,0:T(1,128)}, u32[]{:S(2)}) copy-start(s32[1,192]{1,0:T(1,128)} %param.5) | copy-start | bytes 2308
  3.3 2.8 %copy-start = (bf16[1,192,1024]{2,1,0:T(8,128)(2,1)S(1)}, bf16[1,192,1024]{2,1,0:T(8,128)(2,1)}, u32[]{:S(2)}) copy-start(bf16[1,192,1024]{2,1,0:T(8,128)(2,1)} %param.3) | copy-start | bytes 1179652
  59.8 2.5 %copy-start.1 = (bf16[1,192,1024]{2,1,0:T(8,128)(2,1)S(1)}, bf16[1,192,1024]{2,1,0:T(8,128)(2,1)}, u32[]{:S(2)}) copy-start(bf16[1,192,1024]{2,1,0:T(8,128)(2,1)} %param.4) | copy-start | bytes 1179652
where the time goes:
time: 65.5 us; the launch traced here: 65.1 us
  blocking collectives  53.3 us (81%)
  between operations  4.44 us (7%)
  matrix products  3.55 us (5%)
  local copies, waits for them, and re-layouts  2.14 us (3%)
  other arithmetic  1.7 us (3%)
    psum x1, blocking collectives, local(): lax.psum(partial_sum, ('blk', 'grp')) / (2.0 * total * lax.axis_size('blk'))  41.8 us
    all_gather x2, blocking collectives, merged(): pieces = jax.tree.map(lambda part: lax.all_gather(part, axis), value)  3.64 us
    all_gather x1, blocking collectives, local(): block = lax.all_gather(image, 'grp', axis=1, tiled=True)[0]  2.82 us
    all_gather x1, blocking collectives, local(): piece = lax.all_gather(local_text, 'grp', axis=0, tiled=True)  2.5 us
    unnamed x1, blocking collectives  2.49 us
    unnamed x14, local copies, waits for them, and re-layouts  2.1 us
    dot_general x1, matrix products, local(): summed = jnp.dot(weight_back, piece, preferred_element_type=jnp.float32)  1.69 us
    dot_general x1, matrix products, local(): result = (jnp.dot(weight, block, preferred_element_type=jnp.float32),)  1.33 us

commit v1 on v0

v1 whole, which is shorter than its diff:
```python
import functools

import jax
import jax.numpy as jnp
from jax import lax
from jax.experimental import pallas as pl
from jax.experimental.pallas import tpu as pltpu
from jax.sharding import PartitionSpec as P

score_scale = 0.125
MESH = pl.DeviceIdType.MESH
F32 = jnp.float32


def loop(start, stop, body):
    if stop - start <= 16:
        for number in range(start, stop):
            body(number)
    else:
        pl.loop(start, stop)(body)


def kernel(
    groups,
    blocks,
    text_in,
    image_in,
    pairs_in,
    grad_text,
    grad_image,
    loss,
    text,
    image,
    pairs,
    scores,
    row_exp,
    col_exp,
    row_scale,
    col_scale,
    columns,
    parts,
    out_text,
    out_image,
    load_sem,
    send_sem,
    recv_sem,
    loss_send,
    loss_recv,
    store_sem,
):
    blk = lax.axis_index("blk")
    me = lax.axis_index("grp")
    rows = text_in.shape[1]

    loads = [
        pltpu.make_async_copy(source.at[0], target.at[me], load_sem.at[number])
        for number, (source, target) in enumerate(((image_in, image), (text_in, text)))
    ]
    loads.append(pltpu.make_async_copy(pairs_in, pairs.at[me], load_sem.at[2]))
    for load in loads:
        load.start()

    barrier = pltpu.get_barrier_semaphore()

    def greet_group(step):
        peer = lax.rem(me + step, groups)
        pl.semaphore_signal(barrier, inc=1, device_id={"grp": peer}, device_id_type=MESH)

    def greet_block(step):
        peer = lax.rem(blk + step, blocks)
        pl.semaphore_signal(barrier, inc=1, device_id={"blk": peer}, device_id_type=MESH)

    loop(1, groups, greet_group)
    loop(1, blocks, greet_block)

    def send(kind, buffer, step):
        peer = lax.rem(me + step, groups)
        return pltpu.make_async_remote_copy(
            src_ref=buffer.at[me],
            dst_ref=buffer.at[me],
            send_sem=send_sem.at[kind, step],
            recv_sem=recv_sem.at[kind, step],
            device_id={"grp": peer},
            device_id_type=MESH,
        )

    def arrive(kind, buffer, step):
        source = lax.rem(me - step + groups, groups)
        pltpu.make_async_remote_copy(
            src_ref=buffer.at[source],
            dst_ref=buffer.at[source],
            send_sem=send_sem.at[kind, step],
            recv_sem=recv_sem.at[kind, step],
            device_id={"grp": source},
            device_id_type=MESH,
        ).wait_recv()
        return source

    for load in loads:
        load.wait()
    pl.semaphore_wait(barrier, groups - 1 + blocks - 1)

    buffers = (image, text, pairs)
    for kind, buffer in ((2, pairs), (0, image), (1, text)):
        loop(1, groups, lambda step, kind=kind, buffer=buffer: send(kind, buffer, step).start())

    def score(t, i):
        scores[t, i] = (
            lax.dot_general(
                text[t], image[i], (((1,), (1,)), ((), ())), preferred_element_type=F32
            )
            * score_scale
        )

    score(me, me)

    def pair_step(step):
        arrive(2, pairs, step)

    loop(1, groups, pair_step)
    same = lax.broadcasted_iota(jnp.int32, (rows, rows), 0) == lax.broadcasted_iota(
        jnp.int32, (rows, rows), 1
    )

    def column_step(t):
        values = jnp.broadcast_to(pairs[t].astype(F32), (rows, rows))
        columns[t] = jnp.sum(jnp.where(same, values, 0.0), axis=1, keepdims=True)

    loop(0, groups, column_step)

    def image_step(step):
        score(me, arrive(0, image, step))

    def text_step(step):
        t = arrive(1, text, step)
        loop(0, groups, lambda i: score(t, i))

    loop(1, groups, image_step)
    loop(1, groups, text_step)

    lane = lax.broadcasted_iota(jnp.int32, (rows, rows), 1)

    def hits(t, i):
        return columns[t] == (lane + i * rows).astype(F32)

    def over(count, first, join, value):
        if count <= 8:
            total = first
            for number in range(count):
                total = join(total, value(number))
            return total
        return lax.fori_loop(0, count, lambda n, total: join(total, value(n)), first)

    add = lambda left, right: left + right
    low = -jnp.inf

    def row_step(t, total):
        top = over(
            groups,
            jnp.full((rows, 1), low, F32),
            jnp.maximum,
            lambda i: jnp.max(scores[t, i], axis=1, keepdims=True),
        )

        def term(i):
            value = jnp.exp(scores[t, i] - top)
            row_exp[t, i] = value
            return jnp.sum(value, axis=1, keepdims=True)

        amount = over(groups, jnp.zeros((rows, 1), F32), add, term)
        row_scale[t] = 1.0 / amount
        hit_sum = over(
            groups,
            jnp.zeros((1, rows), F32),
            add,
            lambda i: jnp.sum(jnp.where(hits(t, i), scores[t, i], 0.0), axis=0, keepdims=True),
        )
        return (
            total
            + jnp.sum(top + jnp.log(amount), keepdims=True)
            - 2.0 * jnp.sum(hit_sum, axis=1, keepdims=True)
        )

    def col_step(i, total):
        top = over(
            groups,
            jnp.full((1, rows), low, F32),
            jnp.maximum,
            lambda t: jnp.max(scores[t, i], axis=0, keepdims=True),
        )

        def term(t):
            value = jnp.exp(scores[t, i] - top)
            col_exp[t, i] = value
            return jnp.sum(value, axis=0, keepdims=True)

        amount = over(groups, jnp.zeros((1, rows), F32), add, term)
        col_scale[i] = 1.0 / amount
        return total + jnp.sum(top + jnp.log(amount), axis=1, keepdims=True)

    total = jnp.zeros((1, 1), F32)
    for number in range(groups):
        total = row_step(number, total)
    for number in range(groups):
        total = col_step(number, total)
    parts[blk] = jnp.broadcast_to(total, (1, 128))

    def tell(step):
        peer = lax.rem(blk + step, blocks)
        return pltpu.make_async_remote_copy(
            src_ref=parts.at[blk],
            dst_ref=parts.at[blk],
            send_sem=loss_send.at[step],
            recv_sem=loss_recv.at[step],
            device_id={"blk": peer},
            device_id_type=MESH,
        )

    def hear(step):
        source = lax.rem(blk - step + blocks, blocks)
        pltpu.make_async_remote_copy(
            src_ref=parts.at[source],
            dst_ref=parts.at[source],
            send_sem=loss_send.at[step],
            recv_sem=loss_recv.at[step],
            device_id={"blk": source},
            device_id_type=MESH,
        ).wait_recv()

    loop(1, blocks, lambda step: tell(step).start())

    def weight(t, i):
        return (
            row_exp[t, i] * row_scale[t]
            + col_exp[t, i] * col_scale[i]
            - jnp.where(hits(t, i), 2.0, 0.0)
        ).astype(jnp.bfloat16)

    half = score_scale * 0.5
    grad = jnp.zeros((rows, text_in.shape[2]), F32)
    out_text[...] = (
        over(
            groups,
            grad,
            add,
            lambda i: jnp.dot(weight(me, i), image[i], preferred_element_type=F32),
        )
        * half
    )
    store_text = pltpu.make_async_copy(out_text, grad_text.at[0], store_sem.at[0])
    store_text.start()
    out_image[...] = (
        over(
            groups,
            grad,
            add,
            lambda t: lax.dot_general(
                weight(t, me), text[t], (((0,), (0,)), ((), ())), preferred_element_type=F32
            ),
        )
        * half
    )
    store_image = pltpu.make_async_copy(out_image, grad_image.at[0], store_sem.at[1])
    store_image.start()

    for kind, buffer in enumerate(buffers):
        loop(
            1, groups, lambda step, kind=kind, buffer=buffer: send(kind, buffer, step).wait_send()
        )
    loop(1, blocks, lambda step: tell(step).wait_send())
    loop(1, blocks, hear)
    whole = jnp.sum(parts[...].reshape(blocks, 128), axis=0, keepdims=True)
    loss[...] = whole[:, 0:1] / (2.0 * rows * groups * blocks)
    store_text.wait()
    store_image.wait()


def solution(mesh):
    groups, blocks = mesh.shape["grp"], mesh.shape["blk"]

    def local(text, image, pair_index):
        _, rows, width = text.shape
        anywhere = pl.BlockSpec(memory_space=pl.ANY)
        square = pltpu.VMEM((groups, groups, rows, rows), F32)
        grads_t, grads_i, loss = pl.pallas_call(
            functools.partial(kernel, groups, blocks),
            out_shape=(
                jax.ShapeDtypeStruct(text.shape, F32),
                jax.ShapeDtypeStruct(image.shape, F32),
                jax.ShapeDtypeStruct((1, 1), F32),
            ),
            in_specs=[anywhere] * 3,
            out_specs=(anywhere, anywhere, pl.BlockSpec(memory_space=pltpu.VMEM)),
            scratch_shapes=[
                pltpu.VMEM((groups, rows, width), text.dtype),
                pltpu.VMEM((groups, rows, width), image.dtype),
                pltpu.VMEM((groups, 1, rows), jnp.int32),
                square,
                square,
                square,
                pltpu.VMEM((groups, rows, 1), F32),
                pltpu.VMEM((groups, 1, rows), F32),
                pltpu.VMEM((groups, rows, 1), F32),
                pltpu.VMEM((blocks, 1, 128), F32),
                pltpu.VMEM((rows, width), F32),
                pltpu.VMEM((rows, width), F32),
                pltpu.SemaphoreType.DMA((3,)),
                pltpu.SemaphoreType.DMA((3, groups)),
                pltpu.SemaphoreType.DMA((3, groups)),
                pltpu.SemaphoreType.DMA((blocks,)),
                pltpu.SemaphoreType.DMA((blocks,)),
                pltpu.SemaphoreType.DMA((2,)),
            ],
            compiler_params=pltpu.CompilerParams(collective_id=0, has_side_effects=True),
        )(text, image, pair_index)
        return grads_t, grads_i, loss.reshape(())

    placed = (P("blk", "grp", None), P("blk", "grp", None), P("blk", "grp"))
    return jax.shard_map(
        local,
        mesh=mesh,
        in_specs=placed,
        out_specs=(P("blk", "grp", None), P("blk", "grp", None), P()),
        check_vma=False,
    )
```

time: 65.5 us -> 18.9 us (0.29)
  blocking collectives: 53.3 us -> 0 us
  Pallas kernels: 0 us -> 13.3 us
  matrix products: 3.55 us -> 0 us
  between operations: 4.44 us -> 2.41 us
  other arithmetic: 1.7 us -> 0 us
  local copies, waits for them, and re-layouts: 2.14 us -> 3.04 us
    psum x1 -> x0, blocking collectives: 41.8 us -> none  [local(): lax.psum(partial_sum, ('blk', 'grp')) / (2.0 * total * lax.axis_size('blk'))]
    pallas_call x0 -> x1, Pallas kernels: none -> 13.3 us  [local(): pl.pallas_call(functools.partial(kernel, groups, blocks), out_shape=(jax....]
    all_gather x4 -> x0, blocking collectives: 8.96 us -> none  [the longest x2 3.64 us: merged(): pieces = jax.tree.map(lambda part: lax.all_gather(part, axis), value)]
    dot_general x3 -> x0, matrix products: 3.55 us -> none  [the longest x1 1.69 us: local(): summed = jnp.dot(weight_back, piece, preferred_element_type=jnp.float32)]
    unnamed x1 -> x0, blocking collectives: 2.49 us -> none
    reduce_sum x3 -> x0, other arithmetic: 1.55 us -> none  [the longest x2 1.29 us: local(): partial_sum = jnp.sum(row_lse - 2.0 * positive) + jnp.sum(own_lse)]
    unnamed x14 -> x4, local copies, waits for them, and re-layouts: 2.1 us -> 3.04 us
where the time goes in v1:
time: 18.9 us; the launch traced here: 18.7 us
  Pallas kernels  13.3 us (70%)
  local copies, waits for them, and re-layouts  3.04 us (16%)
  between operations  2.41 us (13%)
    pallas_call x1, Pallas kernels, local(): pl.pallas_call(functools.partial(kernel, groups, blocks), out_shape=(jax....  13.3 us
    unnamed x4, local copies, waits for them, and re-layouts  3.04 us

profile of v1, /device:TPU:0, one launch (start us, length us, event | category | flops | bytes accessed | tf_op | source)
XLA Modules:
  0.0 18.7 jit_solution(6592580895900385400)
XLA Ops:
  0.6 13.3 %shard_map.58 = (f32[1,192,1024]{2,1,0:T(8,128)}, f32[1,192,1024]{2,1,0:T(8,128)}, f32[1,1]{1,0:T(1,128)}) custom-call(bf16[1,192,1024]{2,1,0:T(8,128)(2,1)} %text_in.1, bf16[1,192,1024]{2,1,0:T(8,128)(2,1)} %image_in.1, s32[1,192]{1,0:T(1,128)} %pairs_in.1), custom_call_target="tpu_custom_call" | custom-call | tf_op jit(solution)/shard_map/pallas_call | solution.py:285
  13.9 0.0 copy-start
  13.9 2.2 %copy.9 = f32[1,192,1024]{2,1,0:T(8,128)} copy(f32[1,192,1024]{2,1,0:T(8,128)} %get-tuple-element.12) | data formatting | bytes 1572864
  16.1 0.0 copy-done
  16.1 0.9 %copy.10 = f32[1,192,1024]{2,1,0:T(8,128)} copy(f32[1,192,1024]{2,1,0:T(8,128)S(1)} %copy-done) | data formatting | bytes 1572864
Async XLA Ops:
  13.9 2.2 %copy-start = (f32[1,192,1024]{2,1,0:T(8,128)S(1)}, f32[1,192,1024]{2,1,0:T(8,128)}, u32[]{:S(2)}) copy-start(f32[1,192,1024]{2,1,0:T(8,128)} %get-tuple-element.13) | copy-start | bytes 2359300

commit v2 on v1

--- a/solution.py
+++ b/solution.py
@@ -47,6 +47,7 @@
     loss_send,
     loss_recv,
     store_sem,
+    ready,
 ):
     blk = lax.axis_index("blk")
     me = lax.axis_index("grp")
@@ -61,17 +62,45 @@
         load.start()
 
     barrier = pltpu.get_barrier_semaphore()
-
-    def greet_group(step):
-        peer = lax.rem(me + step, groups)
+    sender = me == 0
+
+    def greet_group(peer):
         pl.semaphore_signal(barrier, inc=1, device_id={"grp": peer}, device_id_type=MESH)
 
     def greet_block(step):
-        peer = lax.rem(blk + step, blocks)
-        pl.semaphore_signal(barrier, inc=1, device_id={"blk": peer}, device_id_type=MESH)
-
-    loop(1, groups, greet_group)
+        pl.semaphore_signal(
+            barrier,
+            inc=1,
+            device_id={"blk": lax.rem(blk + step, blocks), "grp": 0},
+            device_id_type=MESH,
+        )
+
+    @pl.when(sender)
+    def _():
+        loop(1, groups, greet_group)
+
+    @pl.when(jnp.logical_not(sender))
+    def _():
+        pl.semaphore_wait(barrier, 1)
+        pl.semaphore_signal(ready, inc=1, device_id={"grp": 0}, device_id_type=MESH)
+
     loop(1, blocks, greet_block)
+
+    @pl.when(sender)
+    def _():
+        pl.semaphore_wait(ready, groups - 1)
+        if groups > 2:
+
+            def allow(peer):
+                pl.semaphore_signal(ready, inc=1, device_id={"grp": peer}, device_id_type=MESH)
+
+            loop(1, groups, allow)
+
+    if groups > 2:
+
+        @pl.when(jnp.logical_not(sender))
+        def _():
+            pl.semaphore_wait(ready, 1)
 
     def send(kind, buffer, step):
         peer = lax.rem(me + step, groups)
@@ -96,12 +125,9 @@
         ).wait_recv()
         return source
 
-    for load in loads:
-        load.wait()
-    pl.semaphore_wait(barrier, groups - 1 + blocks - 1)
-
     buffers = (image, text, pairs)
     for kind, buffer in ((2, pairs), (0, image), (1, text)):
+        loads[kind].wait()
         loop(1, groups, lambda step, kind=kind, buffer=buffer: send(kind, buffer, step).start())
 
     def score(t, i):
@@ -205,14 +231,13 @@
         total = col_step(number, total)
     parts[blk] = jnp.broadcast_to(total, (1, 128))
 
-    def tell(step):
-        peer = lax.rem(blk + step, blocks)
+    def tell(step, peer):
         return pltpu.make_async_remote_copy(
             src_ref=parts.at[blk],
             dst_ref=parts.at[blk],
-            send_sem=loss_send.at[step],
+            send_sem=loss_send.at[step, peer],
             recv_sem=loss_recv.at[step],
-            device_id={"blk": peer},
+            device_id={"blk": lax.rem(blk + step, blocks), "grp": peer},
             device_id_type=MESH,
         )
 
@@ -221,13 +246,16 @@
         pltpu.make_async_remote_copy(
             src_ref=parts.at[source],
             dst_ref=parts.at[source],
-            send_sem=loss_send.at[step],
+            send_sem=loss_send.at[step, 0],
             recv_sem=loss_recv.at[step],
-            device_id={"blk": source},
+            device_id={"blk": source, "grp": 0},
             device_id_type=MESH,
         ).wait_recv()
 
-    loop(1, blocks, lambda step: tell(step).start())
+    @pl.when(sender)
+    def _():
+        pl.semaphore_wait(barrier, (blocks - 1) * groups)
+        loop(1, blocks, lambda step: loop(0, groups, lambda peer: tell(step, peer).start()))
 
     def weight(t, i):
         return (
@@ -267,7 +295,11 @@
         loop(
             1, groups, lambda step, kind=kind, buffer=buffer: send(kind, buffer, step).wait_send()
         )
-    loop(1, blocks, lambda step: tell(step).wait_send())
+
+    @pl.when(sender)
+    def _():
+        loop(1, blocks, lambda step: loop(0, groups, lambda peer: tell(step, peer).wait_send()))
+
     loop(1, blocks, hear)
     whole = jnp.sum(parts[...].reshape(blocks, 128), axis=0, keepdims=True)
     loss[...] = whole[:, 0:1] / (2.0 * rows * groups * blocks)
@@ -289,7 +321,7 @@
                 jax.ShapeDtypeStruct(image.shape, F32),
                 jax.ShapeDtypeStruct((1, 1), F32),
             ),
-            in_specs=[anywhere] * 3,
+            in_specs=[pl.BlockSpec(memory_space=pltpu.HBM)] * 3,
             out_specs=(anywhere, anywhere, pl.BlockSpec(memory_space=pltpu.VMEM)),
             scratch_shapes=[
                 pltpu.VMEM((groups, rows, width), text.dtype),
@@ -307,12 +339,13 @@
                 pltpu.SemaphoreType.DMA((3,)),
                 pltpu.SemaphoreType.DMA((3, groups)),
                 pltpu.SemaphoreType.DMA((3, groups)),
-                pltpu.SemaphoreType.DMA((blocks,)),
+                pltpu.SemaphoreType.DMA((blocks, groups)),
                 pltpu.SemaphoreType.DMA((blocks,)),
                 pltpu.SemaphoreType.DMA((2,)),
+                pltpu.SemaphoreType.REGULAR,
             ],
-            compiler_params=pltpu.CompilerParams(collective_id=0, has_side_effects=True),
-        )(text, image, pair_index)
+            compiler_params=pltpu.CompilerParams(collective_id=0, has_side_effects=True, vmem_limit_bytes=40 << 20),
+        )(*(pltpu.with_memory_space_constraint(x, pltpu.HBM) for x in (text, image, pair_index)))
         return grads_t, grads_i, loss.reshape(())
 
     placed = (P("blk", "grp", None), P("blk", "grp", None), P("blk", "grp"))

time: 18.9 us -> 17.5 us (0.926)
  local copies, waits for them, and re-layouts: 3.04 us -> 1.76 us
    unnamed x4 -> x2, local copies, waits for them, and re-layouts: 3.04 us -> 1.76 us
where the time goes in v2:
time: 17.5 us; the launch traced here: 17.4 us
  Pallas kernels  13.3 us (76%)
  between operations  2.33 us (13%)
  local copies, waits for them, and re-layouts  1.76 us (10%)
    pallas_call x1, Pallas kernels, local(): pl.pallas_call(functools.partial(kernel, groups, blocks), out_shape=(jax....  13.3 us
    unnamed x2, local copies, waits for them, and re-layouts  1.76 us

profile of v2, /device:TPU:0, one launch (start us, length us, event | category | flops | bytes accessed | tf_op | source)
XLA Modules:
  0.0 17.4 jit_solution(8338361200230422326)
XLA Ops:
  0.6 13.3 %shard_map.58 = (f32[1,192,1024]{2,1,0:T(8,128)S(1)}, f32[1,192,1024]{2,1,0:T(8,128)S(1)}, f32[1,1]{1,0:T(1,128)}) custom-call(bf16[1,192,1024]{2,1,0:T(8,128)(2,1)} %text_in.1, bf16[1,192,1024]{2,1,0:T(8,128)(2,1)} %image_in.1, s32[1,192]{1,0:T(1,128)} %pairs_in.1), custom_call_target="tpu_custom_call" | custom-call | tf_op jit(solution)/shard_map/pallas_call | solution.py:317
  13.9 0.9 %copy.9 = f32[1,192,1024]{2,1,0:T(8,128)} copy(f32[1,192,1024]{2,1,0:T(8,128)S(1)} %get-tuple-element.12) | data formatting | bytes 1572864
  14.8 0.9 %copy.10 = f32[1,192,1024]{2,1,0:T(8,128)} copy(f32[1,192,1024]{2,1,0:T(8,128)S(1)} %get-tuple-element.13) | data formatting | bytes 1572864

commit v3 on v2

--- a/solution.py
+++ b/solution.py
@@ -48,21 +48,29 @@
     loss_recv,
     store_sem,
     ready,
+    terms,
 ):
     blk = lax.axis_index("blk")
     me = lax.axis_index("grp")
     rows = text_in.shape[1]
 
-    loads = [
-        pltpu.make_async_copy(source.at[0], target.at[me], load_sem.at[number])
-        for number, (source, target) in enumerate(((image_in, image), (text_in, text)))
-    ]
-    loads.append(pltpu.make_async_copy(pairs_in, pairs.at[me], load_sem.at[2]))
-    for load in loads:
-        load.start()
+    pieces = 4 if rows % 64 == 0 else 1
+    step_rows = rows // pieces
+    strips = [pl.ds(piece * step_rows, step_rows) for piece in range(pieces)]
 
     barrier = pltpu.get_barrier_semaphore()
     sender = me == 0
+
+    loads = [
+        [
+            pltpu.make_async_copy(
+                source.at[0, strip], target.at[me, strip], load_sem.at[kind, piece]
+            )
+            for piece, strip in enumerate(strips)
+        ]
+        for kind, (source, target) in enumerate(((image_in, image), (text_in, text)))
+    ]
+    loads.append([pltpu.make_async_copy(pairs_in, pairs.at[me], load_sem.at[2, 0])])
 
     def greet_group(peer):
         pl.semaphore_signal(barrier, inc=1, device_id={"grp": peer}, device_id_type=MESH)
@@ -79,6 +87,9 @@
     def _():
         loop(1, groups, greet_group)
 
+    for load in loads[2] + loads[0] + loads[1]:
+        load.start()
+
     @pl.when(jnp.logical_not(sender))
     def _():
         pl.semaphore_wait(barrier, 1)
@@ -102,33 +113,42 @@
         def _():
             pl.semaphore_wait(ready, 1)
 
-    def send(kind, buffer, step):
-        peer = lax.rem(me + step, groups)
+    def views(kind, buffer, owner):
+        if kind == 2:
+            return [buffer.at[owner]]
+        return [buffer.at[owner, strip] for strip in strips]
+
+    def swap(kind, buffer, owner, step, peer, piece):
+        view = views(kind, buffer, owner)[piece]
         return pltpu.make_async_remote_copy(
-            src_ref=buffer.at[me],
-            dst_ref=buffer.at[me],
-            send_sem=send_sem.at[kind, step],
-            recv_sem=recv_sem.at[kind, step],
+            src_ref=view,
+            dst_ref=view,
+            send_sem=send_sem.at[kind, step, piece],
+            recv_sem=recv_sem.at[kind, step, piece],
             device_id={"grp": peer},
             device_id_type=MESH,
         )
 
+    def send(kind, buffer, step, piece):
+        return swap(kind, buffer, me, step, lax.rem(me + step, groups), piece)
+
     def arrive(kind, buffer, step):
         source = lax.rem(me - step + groups, groups)
-        pltpu.make_async_remote_copy(
-            src_ref=buffer.at[source],
-            dst_ref=buffer.at[source],
-            send_sem=send_sem.at[kind, step],
-            recv_sem=recv_sem.at[kind, step],
-            device_id={"grp": source},
-            device_id_type=MESH,
-        ).wait_recv()
+        for piece in range(len(loads[kind])):
+            swap(kind, buffer, source, step, source, piece).wait_recv()
         return source
 
     buffers = (image, text, pairs)
     for kind, buffer in ((2, pairs), (0, image), (1, text)):
-        loads[kind].wait()
-        loop(1, groups, lambda step, kind=kind, buffer=buffer: send(kind, buffer, step).start())
+        for piece, load in enumerate(loads[kind]):
+            load.wait()
+            loop(
+                1,
+                groups,
+                lambda step, kind=kind, buffer=buffer, piece=piece: send(
+                    kind, buffer, step, piece
+                ).start(),
+            )
 
     def score(t, i):
         scores[t, i] = (
@@ -156,13 +176,6 @@
 
     def image_step(step):
         score(me, arrive(0, image, step))
-
-    def text_step(step):
-        t = arrive(1, text, step)
-        loop(0, groups, lambda i: score(t, i))
-
-    loop(1, groups, image_step)
-    loop(1, groups, text_step)
 
     lane = lax.broadcasted_iota(jnp.int32, (rows, rows), 1)
 
@@ -180,7 +193,7 @@
     add = lambda left, right: left + right
     low = -jnp.inf
 
-    def row_step(t, total):
+    def row_step(t):
         top = over(
             groups,
             jnp.full((rows, 1), low, F32),
@@ -201,9 +214,8 @@
             add,
             lambda i: jnp.sum(jnp.where(hits(t, i), scores[t, i], 0.0), axis=0, keepdims=True),
         )
-        return (
-            total
-            + jnp.sum(top + jnp.log(amount), keepdims=True)
+        terms[t] = (
+            jnp.sum(top + jnp.log(amount), keepdims=True)
             - 2.0 * jnp.sum(hit_sum, axis=1, keepdims=True)
         )
 
@@ -224,11 +236,17 @@
         col_scale[i] = 1.0 / amount
         return total + jnp.sum(top + jnp.log(amount), axis=1, keepdims=True)
 
+    def text_step(step):
+        t = arrive(1, text, step)
+        loop(0, groups, lambda i: score(t, i))
+        row_step(t)
+
+    loop(1, groups, image_step)
+    row_step(me)
+    loop(1, groups, text_step)
     total = jnp.zeros((1, 1), F32)
     for number in range(groups):
-        total = row_step(number, total)
-    for number in range(groups):
-        total = col_step(number, total)
+        total = col_step(number, total + terms[number])
     parts[blk] = jnp.broadcast_to(total, (1, 128))
 
     def tell(step, peer):
@@ -292,19 +310,41 @@
     store_image.start()
 
     for kind, buffer in enumerate(buffers):
-        loop(
-            1, groups, lambda step, kind=kind, buffer=buffer: send(kind, buffer, step).wait_send()
-        )
+        for piece in range(len(loads[kind])):
+            loop(
+                1,
+                groups,
+                lambda step, kind=kind, buffer=buffer, piece=piece: send(
+                    kind, buffer, step, piece
+                ).wait_send(),
+            )
 
     @pl.when(sender)
     def _():
         loop(1, blocks, lambda step: loop(0, groups, lambda peer: tell(step, peer).wait_send()))
 
     loop(1, blocks, hear)
-    whole = jnp.sum(parts[...].reshape(blocks, 128), axis=0, keepdims=True)
-    loss[...] = whole[:, 0:1] / (2.0 * rows * groups * blocks)
+    everything = jnp.sum(parts[...].reshape(blocks, 128), axis=0, keepdims=True)
+    loss[...] = everything[:, 0:1] / (2.0 * rows * groups * blocks)
     store_text.wait()
     store_image.wait()
+
+
+def deliver(text_from, image_from, text_to, image_to, sem):
+    half = text_from.shape[1] // 2
+    copies = [
+        pltpu.make_async_copy(
+            source.at[0, pl.ds(part * half, half)],
+            target.at[0, pl.ds(part * half, half)],
+            sem.at[kind, part],
+        )
+        for part in range(2)
+        for kind, (source, target) in enumerate(((text_from, text_to), (image_from, image_to)))
+    ]
+    for copy in copies:
+        copy.start()
+    for copy in copies:
+        copy.wait()
 
 
 def solution(mesh):
@@ -336,16 +376,28 @@
                 pltpu.VMEM((blocks, 1, 128), F32),
                 pltpu.VMEM((rows, width), F32),
                 pltpu.VMEM((rows, width), F32),
-                pltpu.SemaphoreType.DMA((3,)),
-                pltpu.SemaphoreType.DMA((3, groups)),
-                pltpu.SemaphoreType.DMA((3, groups)),
+                pltpu.SemaphoreType.DMA((3, 4)),
+                pltpu.SemaphoreType.DMA((3, groups, 4)),
+                pltpu.SemaphoreType.DMA((3, groups, 4)),
                 pltpu.SemaphoreType.DMA((blocks, groups)),
                 pltpu.SemaphoreType.DMA((blocks,)),
                 pltpu.SemaphoreType.DMA((2,)),
                 pltpu.SemaphoreType.REGULAR,
+                pltpu.VMEM((groups, 1, 1), F32),
             ],
             compiler_params=pltpu.CompilerParams(collective_id=0, has_side_effects=True, vmem_limit_bytes=40 << 20),
         )(*(pltpu.with_memory_space_constraint(x, pltpu.HBM) for x in (text, image, pair_index)))
+        grads_t, grads_i = pl.pallas_call(
+            deliver,
+            out_shape=(
+                jax.ShapeDtypeStruct(text.shape, F32),
+                jax.ShapeDtypeStruct(image.shape, F32),
+            ),
+            in_specs=[anywhere] * 2,
+            out_specs=(pl.BlockSpec(memory_space=pltpu.HBM),) * 2,
+            scratch_shapes=[pltpu.SemaphoreType.DMA((2, 2))],
+            compiler_params=pltpu.CompilerParams(vmem_limit_bytes=1 << 20),
+        )(grads_t, grads_i)
         return grads_t, grads_i, loss.reshape(())
 
     placed = (P("blk", "grp", None), P("blk", "grp", None), P("blk", "grp"))

time: 17.5 us -> 17.5 us (level)
  local copies, waits for them, and re-layouts: 1.76 us -> 0 us
  Pallas kernels: 13.3 us -> 15 us
    unnamed x2 -> x0, local copies, waits for them, and re-layouts: 1.76 us -> none
    pallas_call x0 -> x1, Pallas kernels: none -> 1.17 us  [local(): pl.pallas_call(deliver, out_shape=(jax.ShapeDtypeStruct(text.shape, F32),...]
    pallas_call x1, Pallas kernels: 13.3 us -> 13.8 us  [local(): pl.pallas_call(functools.partial(kernel, groups, blocks), out_shape=(jax....]
where the time goes in v3:
time: 17.5 us; the launch traced here: 17.4 us
  Pallas kernels  15 us (86%)
  between operations  2.4 us (14%)
    pallas_call x1, Pallas kernels, local(): pl.pallas_call(functools.partial(kernel, groups, blocks), out_shape=(jax....  13.8 us
    pallas_call x1, Pallas kernels, local(): pl.pallas_call(deliver, out_shape=(jax.ShapeDtypeStruct(text.shape, F32),...  1.17 us

profile of v3, /device:TPU:0, one launch (start us, length us, event | category | flops | bytes accessed | tf_op | source)
XLA Modules:
  0.0 17.4 jit_solution(631454869212965931)
XLA Ops:
  0.6 13.8 %shard_map.58 = (f32[1,192,1024]{2,1,0:T(8,128)S(1)}, f32[1,192,1024]{2,1,0:T(8,128)S(1)}, f32[1,1]{1,0:T(1,128)}) custom-call(bf16[1,192,1024]{2,1,0:T(8,128)(2,1)} %text_in.1, bf16[1,192,1024]{2,1,0:T(8,128)(2,1)} %image_in.1, s32[1,192]{1,0:T(1,128)} %pairs_in.1), custom_call_target="tpu_custom_call" | custom-call | tf_op jit(solution)/shard_map/pallas_call | solution.py:357
  14.4 1.2 %shard_map.59 = (f32[1,192,1024]{2,1,0:T(8,128)}, f32[1,192,1024]{2,1,0:T(8,128)}) custom-call(f32[1,192,1024]{2,1,0:T(8,128)S(1)} %get-tuple-element.8.text_from, f32[1,192,1024]{2,1,0:T(8,128)S(1)} %get-tuple-element.9.image_from), custom_call_target="tpu_custom_call" | custom-call | tf_op jit(solution)/shard_map/pallas_call | solution.py:390

commit v4 on v2

--- a/solution.py
+++ b/solution.py
@@ -28,7 +28,7 @@
     pairs_in,
     grad_text,
     grad_image,
-    loss,
+    parts,
     text,
     image,
     pairs,
@@ -38,7 +38,7 @@
     row_scale,
     col_scale,
     columns,
-    parts,
+    mine,
     out_text,
     out_image,
     load_sem,
@@ -105,7 +105,7 @@
     def send(kind, buffer, step):
         peer = lax.rem(me + step, groups)
         return pltpu.make_async_remote_copy(
-            src_ref=buffer.at[me],
+            src_ref=(image_in.at[0], text_in.at[0], pairs_in)[kind],
             dst_ref=buffer.at[me],
             send_sem=send_sem.at[kind, step],
             recv_sem=recv_sem.at[kind, step],
@@ -127,8 +127,9 @@
 
     buffers = (image, text, pairs)
     for kind, buffer in ((2, pairs), (0, image), (1, text)):
-        loads[kind].wait()
         loop(1, groups, lambda step, kind=kind, buffer=buffer: send(kind, buffer, step).start())
+    for load in loads:
+        load.wait()
 
     def score(t, i):
         scores[t, i] = (
@@ -229,11 +230,11 @@
         total = row_step(number, total)
     for number in range(groups):
         total = col_step(number, total)
-    parts[blk] = jnp.broadcast_to(total, (1, 128))
+    mine[...] = jnp.broadcast_to(total, (1, 128))
 
     def tell(step, peer):
         return pltpu.make_async_remote_copy(
-            src_ref=parts.at[blk],
+            src_ref=mine,
             dst_ref=parts.at[blk],
             send_sem=loss_send.at[step, peer],
             recv_sem=loss_recv.at[step],
@@ -256,6 +257,9 @@
     def _():
         pl.semaphore_wait(barrier, (blocks - 1) * groups)
         loop(1, blocks, lambda step: loop(0, groups, lambda peer: tell(step, peer).start()))
+
+    keep = pltpu.make_async_copy(mine, parts.at[blk], store_sem.at[2])
+    keep.start()
 
     def weight(t, i):
         return (
@@ -301,10 +305,36 @@
         loop(1, blocks, lambda step: loop(0, groups, lambda peer: tell(step, peer).wait_send()))
 
     loop(1, blocks, hear)
-    whole = jnp.sum(parts[...].reshape(blocks, 128), axis=0, keepdims=True)
-    loss[...] = whole[:, 0:1] / (2.0 * rows * groups * blocks)
+    keep.wait()
     store_text.wait()
     store_image.wait()
+
+
+def deliver(
+    pairs_total, text_from, image_from, parts_from, text_to, image_to, loss_to, parts, loss, sem
+):
+    half = text_from.shape[1] // 2
+    copies = [
+        pltpu.make_async_copy(
+            source.at[0, pl.ds(part * half, half)],
+            target.at[0, pl.ds(part * half, half)],
+            sem.at[kind, part],
+        )
+        for part in range(2)
+        for kind, (source, target) in enumerate(((text_from, text_to), (image_from, image_to)))
+    ]
+    fetch = pltpu.make_async_copy(parts_from, parts, sem.at[2, 0])
+    fetch.start()
+    for copy in copies:
+        copy.start()
+    fetch.wait()
+    total = jnp.sum(parts[...].reshape(parts.shape[0], 128), axis=0, keepdims=True)
+    loss[...] = total[:, 0:1] / (2.0 * pairs_total)
+    put = pltpu.make_async_copy(loss, loss_to, sem.at[2, 1])
+    put.start()
+    for copy in copies:
+        copy.wait()
+    put.wait()
 
 
 def solution(mesh):
@@ -314,15 +344,15 @@
         _, rows, width = text.shape
         anywhere = pl.BlockSpec(memory_space=pl.ANY)
         square = pltpu.VMEM((groups, groups, rows, rows), F32)
-        grads_t, grads_i, loss = pl.pallas_call(
+        grads_t, grads_i, parts = pl.pallas_call(
             functools.partial(kernel, groups, blocks),
             out_shape=(
                 jax.ShapeDtypeStruct(text.shape, F32),
                 jax.ShapeDtypeStruct(image.shape, F32),
-                jax.ShapeDtypeStruct((1, 1), F32),
+                jax.ShapeDtypeStruct((blocks, 1, 128), F32),
             ),
             in_specs=[pl.BlockSpec(memory_space=pltpu.HBM)] * 3,
-            out_specs=(anywhere, anywhere, pl.BlockSpec(memory_space=pltpu.VMEM)),
+            out_specs=(anywhere,) * 3,
             scratch_shapes=[
                 pltpu.VMEM((groups, rows, width), text.dtype),
                 pltpu.VMEM((groups, rows, width), image.dtype),
@@ -333,7 +363,7 @@
                 pltpu.VMEM((groups, rows, 1), F32),
                 pltpu.VMEM((groups, 1, rows), F32),
                 pltpu.VMEM((groups, rows, 1), F32),
-                pltpu.VMEM((blocks, 1, 128), F32),
+                pltpu.VMEM((1, 128), F32),
                 pltpu.VMEM((rows, width), F32),
                 pltpu.VMEM((rows, width), F32),
                 pltpu.SemaphoreType.DMA((3,)),
@@ -341,11 +371,27 @@
                 pltpu.SemaphoreType.DMA((3, groups)),
                 pltpu.SemaphoreType.DMA((blocks, groups)),
                 pltpu.SemaphoreType.DMA((blocks,)),
-                pltpu.SemaphoreType.DMA((2,)),
+                pltpu.SemaphoreType.DMA((3,)),
                 pltpu.SemaphoreType.REGULAR,
             ],
             compiler_params=pltpu.CompilerParams(collective_id=0, has_side_effects=True, vmem_limit_bytes=40 << 20),
         )(*(pltpu.with_memory_space_constraint(x, pltpu.HBM) for x in (text, image, pair_index)))
+        grads_t, grads_i, loss = pl.pallas_call(
+            functools.partial(deliver, rows * groups * blocks),
+            out_shape=(
+                jax.ShapeDtypeStruct(text.shape, F32),
+                jax.ShapeDtypeStruct(image.shape, F32),
+                jax.ShapeDtypeStruct((1, 1), F32),
+            ),
+            in_specs=[anywhere] * 3,
+            out_specs=(pl.BlockSpec(memory_space=pltpu.HBM),) * 3,
+            scratch_shapes=[
+                pltpu.VMEM((blocks, 1, 128), F32),
+                pltpu.VMEM((1, 1), F32),
+                pltpu.SemaphoreType.DMA((3, 2)),
+            ],
+            compiler_params=pltpu.CompilerParams(vmem_limit_bytes=1 << 20),
+        )(grads_t, grads_i, parts)
         return grads_t, grads_i, loss.reshape(())
 
     placed = (P("blk", "grp", None), P("blk", "grp", None), P("blk", "grp"))

time: 17.5 us -> 14.7 us (0.84)
  local copies, waits for them, and re-layouts: 1.76 us -> 0 us
  between operations: 2.33 us -> 0.64 us
  Pallas kernels: 13.3 us -> 13.9 us
    unnamed x2 -> x0, local copies, waits for them, and re-layouts: 1.76 us -> none
    pallas_call x0 -> x1, Pallas kernels: none -> 1.2 us  [local(): pl.pallas_call(functools.partial(deliver, rows * groups * blocks), out_sh...]
    pallas_call x1, Pallas kernels: 13.3 us -> 12.7 us  [local(): pl.pallas_call(functools.partial(kernel, groups, blocks), out_shape=(jax....]
where the time goes in v4:
time: 14.7 us; the launch traced here: 14.5 us
  Pallas kernels  13.9 us (95%)
  between operations  0.64 us (4%)
    pallas_call x1, Pallas kernels, local(): pl.pallas_call(functools.partial(kernel, groups, blocks), out_shape=(jax....  12.7 us
    pallas_call x1, Pallas kernels, local(): pl.pallas_call(functools.partial(deliver, rows * groups * blocks), out_sh...  1.2 us

profile of v4, /device:TPU:0, one launch (start us, length us, event | category | flops | bytes accessed | tf_op | source)
XLA Modules:
  0.0 14.5 jit_solution(10382556836268085233)
XLA Ops:
  0.6 12.7 %shard_map.58 = (f32[1,192,1024]{2,1,0:T(8,128)S(1)}, f32[1,192,1024]{2,1,0:T(8,128)S(1)}, f32[16,1,128]{2,1,0:T(1,128)S(1)}) custom-call(bf16[1,192,1024]{2,1,0:T(8,128)(2,1)} %text_in.1, bf16[1,192,1024]{2,1,0:T(8,128)(2,1)} %image_in.1, s32[1,192]{1,0:T(1,128)} %pairs_in.1), custom_call_target="tpu_custom_call" | custom-call | tf_op jit(solution)/shard_map/pallas_call | solution.py:347
  13.3 1.2 %shard_map.59 = (f32[1,192,1024]{2,1,0:T(8,128)}, f32[1,192,1024]{2,1,0:T(8,128)}, f32[1,1]{1,0:T(1,128)}) custom-call(f32[1,192,1024]{2,1,0:T(8,128)S(1)} %get-tuple-element.9.text_from, f32[1,192,1024]{2,1,0:T(8,128)S(1)} %get-tuple-element.10.image_from, f32[16,1,128]{2,1,0:T(1,128)S(1)} %get-tuple-element.11.parts_from), custom_call_target="tpu_custom_call" | custom-call | tf_op jit(solution)/shard_map/pallas_call | solution.py:379
